TPU v7x, 32 devices: a whole 2x2x4 slice. The times are simulated.
32 devices in a mesh: row: 4 (over x, core), col: 8 (over z, y).
Axes of the slice: x: 2, y: 2, z: 4, core: 2. Of those that a mesh axis runs over, the one named last changes fastest.
Arguments:
- rhs_c: float32 [12, 512, 6, 1024], P(None, 'row', None, 'col'), may hold values from -6 to 6
- rhs_f: float32 [12, 512, 6, 1024], P(None, 'row', None, 'col'), may hold values from -6 to 6
- pencil_a: bfloat16 [12, 512, 6, 1024], P(None, 'row', None, 'col'), may hold values from -0.5 to 0.5
- pencil_d: bfloat16 [12, 512, 6, 1024], P(None, 'row', None, 'col'), may hold values from -0.5 to 0.5
- pencil_b: bfloat16 [12, 512, 6, 1024], P(None, 'row', None, 'col'), may hold values from -0.5 to 0.5
- pencil_e: bfloat16 [12, 512, 6, 1024], P(None, 'row', None, 'col'), may hold values from -0.5 to 0.5
- d_inverse: float32 [12, 512, 128], P(None, 'row'), may hold values from -0.25 to 2.5
- left_vectors: float32 [12, 512, 128], P(None, 'row'), may hold values from -0.25 to 2.5
- left_inverse: float32 [12, 512, 128], P(None, 'row'), may hold values from -0.25 to 2.5
- left_eigs: float32 [12, 512], P(None, 'row'), may hold values from 1 to 3
- e_inverse: float32 [6, 1024, 128], P(None, 'col'), may hold values from -0.25 to 2.5
- right_vectors: float32 [6, 1024, 128], P(None, 'col'), may hold values from -0.25 to 2.5
- right_inverse: float32 [6, 1024, 128], P(None, 'col'), may hold values from -0.25 to 2.5
- right_eigs: float32 [6, 1024], P(None, 'col'), may hold values from -3 to -1
Outputs:
- updated_c: float32 [12, 512, 6, 1024], P(None, 'row', None, 'col')
- updated_f: float32 [12, 512, 6, 1024], P(None, 'row', None, 'col')
- solved_r: float32 [12, 512, 6, 1024], P(None, 'row', None, 'col')
- solved_l: float32 [12, 512, 6, 1024], P(None, 'row', None, 'col')
All inputs are finite; a program needn't handle non-finite values.
Results may differ from a plain program's by a relative error of at most 0.0003.
Values may be sent and summed in bfloat16 or wider, within the bound.
A program may use at most 128 MiB of HBM per device.

v0:
```python
import functools

import jax
import jax.numpy as jnp
from jax import lax
from jax.experimental import pallas as pl
from jax.experimental.pallas import tpu as pltpu
from jax.sharding import PartitionSpec as P

TILE = 128
PIECES = 3


def product(left, right):
    return jnp.einsum("bij,bjk->bik", left, right, precision=lax.Precision.HIGHEST)


def half_product(exact, value):
    hi, lo = split(value)
    dot = functools.partial(jnp.einsum, "bij,bjk->bik", preferred_element_type=jnp.float32)
    return dot(exact, hi) + dot(exact, lo)


def product_half(value, exact):
    hi, lo = split(value)
    dot = functools.partial(jnp.einsum, "bij,bjk->bik", preferred_element_type=jnp.float32)
    return dot(hi, exact) + dot(lo, exact)


def split(value):
    hi = lax.reduce_precision(value, 8, 7)
    return hi.astype(jnp.bfloat16), (value - hi).astype(jnp.bfloat16)


def heights(rows_dev, cols_dev, count_rows, count_cols):
    return [min(rows_dev, (b * count_cols + count_cols - 1) // count_rows + 1) for b in range(cols_dev)]


def pack(left, right, tall):
    tiles = [jnp.stack([left[:n, b], right[:n, b]]) for b, n in enumerate(tall)]
    return jnp.concatenate(tiles, axis=1)


def update_kernel(
    count_rows, count_cols, place, c_ref, f_ref, a_ref, d_ref, b_ref, e_ref, r_ref, l_ref, ad_ref, be_ref, c_out, f_out
):
    a = pl.program_id(0)
    row, col = place[0], place[1]
    cols_dev = c_ref.shape[1]
    total = ad_ref.shape[2]
    i = a * count_rows + row
    col_side, row_side = lax.rem(col, 2), lax.rem(row, 2)
    for b in range(cols_dev):
        j = b * count_cols + col

        @pl.when(i > j)
        def _():
            c_out[0, b] = c_ref[0, b]
            f_out[0, b] = f_ref[0, b]

        @pl.when(i <= j)
        def _():
            slot_right = jnp.minimum(b + (col == count_cols - 1).astype(jnp.int32), cols_dev - 1)
            slot_left = jnp.maximum(b - (col == 0).astype(jnp.int32), 0)
            right = jnp.clip(place[2 + slot_right] + a, 0, total - 1)
            left = jnp.clip(place[2 + slot_left] + a, 0, total - 1)
            up = jnp.clip(place[2 + b] + a - (row == 0).astype(jnp.int32), 0, total - 1)
            down = jnp.clip(place[2 + b] + a + (row == count_rows - 1).astype(jnp.int32), 0, total - 1)
            keep_mid = jnp.full((TILE, TILE), jnp.where(i < j, 1.0, 0.0), jnp.float32).astype(jnp.bfloat16)
            keep_far = jnp.full((TILE, TILE), jnp.where(i < j - 1, 1.0, 0.0), jnp.float32).astype(jnp.bfloat16)

            def wide(which, own):
                return jnp.concatenate(
                    [ad_ref[col_side, which, right], own * keep_mid, ad_ref[1 - col_side, which, left] * keep_far], axis=1
                )

            lhs = jnp.concatenate([wide(0, a_ref[0, b]), wide(1, d_ref[0, b])], axis=0)
            first = jnp.dot(lhs, r_ref[b], preferred_element_type=jnp.float32)

            def tall(which, own):
                return jnp.concatenate(
                    [be_ref[1 - row_side, which, up], own * keep_mid, be_ref[row_side, which, down] * keep_far], axis=0
                )

            rhs = jnp.concatenate([tall(0, b_ref[0, b]), tall(1, e_ref[0, b])], axis=1)
            second = jnp.dot(l_ref[0], rhs, preferred_element_type=jnp.float32)
            c_out[0, b] = (
                c_ref[0, b]
                - (first[:TILE, :TILE] + first[:TILE, TILE:])
                + (second[:TILE, :TILE] + second[TILE:, :TILE])
            )
            f_out[0, b] = (
                f_ref[0, b]
                - (first[TILE:, :TILE] + first[TILE:, TILE:])
                + (second[:TILE, TILE:] + second[TILE:, TILE:])
            )


def body(
    rhs_c,
    rhs_f,
    pencil_a,
    pencil_d,
    pencil_b,
    pencil_e,
    d_inverse,
    left_vectors,
    left_inverse,
    left_eigs,
    e_inverse,
    right_vectors,
    right_inverse,
    right_eigs,
):
    count_rows = lax.axis_size("row")
    count_cols = lax.axis_size("col")
    row = lax.axis_index("row")
    col = lax.axis_index("col")
    c, f, a, d, b, e = [
        x.transpose(0, 2, 1, 3) for x in (rhs_c, rhs_f, pencil_a, pencil_d, pencil_b, pencil_e)
    ]
    rows_dev, cols_dev = c.shape[:2]
    blocks = rows_dev * count_rows
    slots = jnp.arange(cols_dev, dtype=jnp.int32)
    block_cols = slots * count_cols + col
    tall = heights(rows_dev, cols_dev, count_rows, count_cols)
    offsets = [sum(tall[:k]) for k in range(cols_dev)]

    def shift(value, axis, by):
        n = lax.axis_size(axis)
        return lax.ppermute(value, axis, [(k, (k + by) % n) for k in range(n)])

    band = jnp.clip((block_cols - row) // count_rows, 0, rows_dev - 1)
    band_ad = jnp.stack([a[band, slots], d[band, slots]])
    band_be = jnp.stack([b[band, slots], e[band, slots]])
    from_right = shift(band_ad, "col", -1)
    from_left = shift(band_ad[0], "col", 1)
    from_up = shift(band_be, "row", 1)
    from_down = shift(band_be[1], "row", -1)
    from_right = jnp.where(col == count_cols - 1, jnp.roll(from_right, -1, axis=1), from_right)
    from_left = jnp.where(col == 0, jnp.roll(from_left, 1, axis=0), from_left)

    pack_ad = pack(a, d, tall)
    pack_be = pack(b, e, tall)
    total = pack_ad.shape[1]
    pieces = min(PIECES, total)
    cuts = [total * k // pieces for k in range(pieces + 1)]
    swap_col = [(k, k ^ 1) for k in range(count_cols)]
    relay_col = [(k, (k + 2 if k % 2 == 0 else k - 2) % count_cols) for k in range(count_cols)]
    swap_row = [(k, k ^ 1) for k in range(count_rows)]
    cross_row = [(k, (k - 1 if k % 2 == 0 else k + 1) % count_rows) for k in range(count_rows)]
    swapped, relayed = [], []
    for lo, hi in zip(cuts[:-1], cuts[1:]):
        got = lax.ppermute(pack_ad[:, lo:hi], "col", swap_col)
        swapped.append(got)
        relayed.append(lax.ppermute(got, "col", relay_col))
    be_swap = lax.ppermute(pack_be, "row", swap_row)
    be_cross = lax.ppermute(pack_be, "row", cross_row)
    near_ad = jnp.stack([jnp.concatenate(swapped, axis=1), jnp.concatenate(relayed, axis=1)])
    near_be = jnp.stack([be_swap, be_cross])

    phase = (col - row) % count_rows
    ahead = phase == count_rows - 1
    level = phase == 0
    behind = phase == 1
    mine = (block_cols + 1 - row) // count_rows
    front_rows = mine * count_rows + row
    valid = (ahead | level | behind) & (front_rows >= 0) & (front_rows < blocks)
    mine = jnp.clip(mine, 0, rows_dev - 1)
    front_c = c[mine, slots]
    front_f = f[mine, slots]
    own_a, own_d, own_b, own_e = [x[mine, slots] for x in (a, d, b, e)]
    a_diag = jnp.where(ahead, from_right[0], jnp.where(level, own_a, from_left)).astype(jnp.float32)
    e_diag = jnp.where(ahead, from_up[1], jnp.where(level, own_e, from_down)).astype(jnp.float32)
    inv_d, vec_left, back_left = d_inverse[mine], left_vectors[mine], left_inverse[mine]
    spread = left_eigs[mine][:, :, None] - right_eigs[:, None, :]
    coupled = product(a_diag, inv_d)

    def solve(resid_c, resid_f):
        merged = product(resid_c - product(coupled, resid_f), e_inverse)
        spectral = product(product(back_left, merged), right_vectors) / spread
        new_l = product(product(vec_left, spectral), right_inverse)
        new_r = product(inv_d, resid_f + product(new_l, e_diag))
        keep = valid[:, None, None]
        return jnp.where(keep, new_r, 0.0), jnp.where(keep, new_l, 0.0)

    def onward(value, by):
        got = shift(value, "col", by)
        moved = jnp.concatenate([jnp.zeros_like(got[:1]), got[:-1]])
        return jnp.where(col < by, moved, got)

    r_one, l_one = solve(front_c, front_f)
    r_in, l_in = shift(r_one, "row", -1), onward(l_one, 1)
    r_far, l_far = shift(r_one, "row", -2), onward(l_one, 2)
    r_two, l_two = solve(
        front_c - half_product(from_right[0], r_in) + product_half(l_in, from_up[0]),
        front_f - half_product(from_right[1], r_in) + product_half(l_in, from_up[1]),
    )
    base_c = front_c - half_product(from_right[0], r_far) + product_half(l_far, from_up[0])
    base_f = front_f - half_product(from_right[1], r_far) + product_half(l_far, from_up[1])
    r_in, l_in = shift(r_two, "row", -1), onward(l_two, 1)
    r_three, l_three = solve(
        base_c - half_product(own_a, r_in) + product_half(l_in, own_b),
        base_f - half_product(own_d, r_in) + product_half(l_in, own_e),
    )
    new_r = jnp.where(ahead, r_one, jnp.where(level, r_two, r_three))
    new_l = jnp.where(ahead, l_one, jnp.where(level, l_two, l_three))

    every_r = lax.all_gather(new_r, "row")
    every_l = lax.all_gather(new_l, "col")
    r_parts, l_parts = [], []
    block_rows = jnp.arange(rows_dev, dtype=jnp.int32) * count_rows + row
    for offset in (1, 0, -1):
        r_parts.append(every_r[(col + offset) % count_rows])
        at = block_rows - offset
        inside = (at >= 0) & (at < blocks)
        at = jnp.clip(at, 0, blocks - 1)
        l_parts.append(jnp.where(inside[:, None, None], every_l[at % count_cols, at // count_cols], 0.0))
    r_all = jnp.concatenate(split(jnp.concatenate(r_parts, axis=1)), axis=2)
    l_all = jnp.concatenate(split(jnp.concatenate(l_parts, axis=2)), axis=1)

    place = jnp.concatenate([jnp.stack([row, col]).astype(jnp.int32), jnp.array(offsets, jnp.int32)])
    line = pl.BlockSpec((1, cols_dev, TILE, TILE), lambda k: (k, 0, 0, 0))
    whole = pl.BlockSpec(memory_space=pltpu.VMEM)
    new_c, new_f = pl.pallas_call(
        functools.partial(update_kernel, count_rows, count_cols),
        grid=(rows_dev,),
        in_specs=[pl.BlockSpec(memory_space=pltpu.SMEM)]
        + [line] * 6
        + [whole, pl.BlockSpec((1, 2 * TILE, 3 * TILE), lambda k: (k, 0, 0)), whole, whole],
        out_specs=[line, line],
        out_shape=[jax.ShapeDtypeStruct(c.shape, jnp.float32)] * 2,
        compiler_params=pltpu.CompilerParams(vmem_limit_bytes=48 * 1024 * 1024),
        name="update",
    )(place, c, f, a, d, b, e, r_all, l_all, near_ad, near_be)

    here = (valid[None, :] & (jnp.arange(rows_dev, dtype=jnp.int32)[:, None] == mine[None, :]))[:, :, None, None]
    out_r = jnp.where(here, new_r[None], 0.0)
    out_l = jnp.where(here, new_l[None], 0.0)
    return tuple(x.transpose(0, 2, 1, 3) for x in (new_c, new_f, out_r, out_l))


def solution(mesh):
    grid = P(None, "row", None, "col")
    left, right = P(None, "row", None), P(None, "col", None)
    in_specs = (grid,) * 6 + (left,) * 3 + (P(None, "row"),) + (right,) * 3 + (P(None, "col"),)
    return jax.shard_map(body, mesh=mesh, in_specs=in_specs, out_specs=(grid,) * 4, check_vma=False)
```

profile of v0, /device:TPU:28, one launch (start us, length us, event | category | flops | bytes accessed | tf_op | source)
XLA Modules:
  0.0 326.4 jit_solution(10624039737499645998)
XLA Ops:
  7.2 3.5 %copy.46 = bf16[12,128,6,128]{3,1,0,2:T(8,128)(2,1)} copy(bf16[12,128,6,128]{3,1,2,0:T(8,128)(2,1)} %param.17) | data formatting | bytes 4718592 | tf_op args[2]
  10.8 3.0 gather_fusion.5
  15.4 2.3 gather_fusion.6
  21.4 3.4 %copy.43 = bf16[12,128,6,128]{3,1,0,2:T(8,128)(2,1)} copy(bf16[12,128,6,128]{3,1,2,0:T(8,128)(2,1)} %param.20) | data formatting | bytes 4718592 | tf_op args[5]
  24.8 2.9 gather_fusion.10
  28.1 3.3 %copy.44 = bf16[12,128,6,128]{3,1,0,2:T(8,128)(2,1)} copy(bf16[12,128,6,128]{3,1,2,0:T(8,128)(2,1)} %param.19) | data formatting | bytes 4718592 | tf_op args[4]
  31.5 2.3 gather_fusion.9
  41.9 3.0 gather_fusion.7
  44.9 2.9 gather_fusion.11
  47.8 3.7 %gather_fusion.1 = f32[6,128,128]{2,1,0:T(8,128)} fusion(f32[12,6,128,128]{3,2,1,0:T(8,128)} %bitcast.238, s32[6]{0:T(128)S(1)} %or_bitcast_fusion), kind=kCustom, calls=%fused_computation.1 | custom fusion | bytes 786480 | tf_op jit(solution)/shard_map/gather | solution.py:171
  51.5 3.7 %gather_fusion.4 = f32[6,128,128]{2,1,0:T(8,128)} fusion(f32[12,6,128,128]{3,2,1,0:T(8,128)} %bitcast.236, s32[6]{0:T(128)S(1)} %or_bitcast_fusion), kind=kCustom, calls=%fused_computation.4 | custom fusion | bytes 786480 | tf_op jit(solution)/shard_map/gather | solution.py:170
  55.8 2.4 gather_fusion.3
  59.3 2.5 gather_fusion.2
  77.9 3.1 collective-permute-start.5
  81.6 3.0 gather_fusion.13
  84.6 3.0 gather_fusion.12
  114.5 5.6 %collective-permute-done.9 = f32[6,128,128]{2,1,0:T(8,128)S(1)} collective-permute-done((f32[6,128,128]{2,1,0:T(8,128)S(1)}, f32[6,128,128]{2,1,0:T(8,128)S(1)}, u32[]{:S(2)}, u32[]{:S(2)}) %collective-permute-start.9) | collective-permute-done | bytes 393248 | tf_op jit(solution)/shard_map/ppermute | solution.py:131
  126.9 2.3 fusion.16
  154.9 24.0 %collective-permute-done.10 = bf16[2,14,128,128]{3,2,1,0:T(8,128)(2,1)} collective-permute-done((bf16[2,14,128,128]{3,2,1,0:T(8,128)(2,1)S(1)}, bf16[2,14,128,128]{3,2,1,0:T(8,128)(2,1)}, u32[]{:S(2)}, u32[]{:S(2)}) %collective-permute-start.10) | collective-permute-done | bytes 917536 | tf_op jit(solution)/shard_map/ppermute | solution.py:154
  178.8 2.4 collective-permute-start.13
  181.2 23.4 %collective-permute-done.11 = bf16[2,14,128,128]{3,2,1,0:T(8,128)(2,1)} collective-permute-done((bf16[2,14,128,128]{3,2,1,0:T(8,128)(2,1)S(1)}, bf16[2,14,128,128]{3,2,1,0:T(8,128)(2,1)}, u32[]{:S(2)}, u32[]{:S(2)}) %collective-permute-start.11) | collective-permute-done | bytes 917536 | tf_op jit(solution)/shard_map/ppermute | solution.py:154
  204.6 4.3 %collective-permute-start.14 = (bf16[2,14,128,128]{3,2,1,0:T(8,128)(2,1)}, bf16[2,14,128,128]{3,2,1,0:T(8,128)(2,1)}, u32[]{:S(2)}, u32[]{:S(2)}) collective-permute-start(bf16[2,14,128,128]{3,2,1,0:T(8,128)(2,1)} %collective-permute-done.11), channel_id=1, source_target_pairs={{0,2},{1,7},{2,4},{3,1},{4,6},{5,3},{6,0},{7,5},{8,10},{9,15},{10,... | collective-permute-start | bytes 2752520 | tf_op jit(solution)/shard_map/ppermute | solution.py:156
  208.9 25.7 %collective-permute-done.12 = bf16[2,14,128,128]{3,2,1,0:T(8,128)(2,1)} collective-permute-done((bf16[2,14,128,128]{3,2,1,0:T(8,128)(2,1)S(1)}, bf16[2,14,128,128]{3,2,1,0:T(8,128)(2,1)}, u32[]{:S(2)}, u32[]{:S(2)}) %collective-permute-start.12) | collective-permute-done | bytes 917536 | tf_op jit(solution)/shard_map/ppermute | solution.py:154
  238.7 4.9 %broadcast_select_fusion = (f32[12,128,6,128]{3,1,2,0:T(8,128)}, f32[12,128,6,128]{3,1,2,0:T(8,128)}) fusion(f32[128,6,128]{2,0,1:T(8,128)S(1)} %bitcast.240, pred[12,6]{1,0:T(8,128)(4,1)S(1)} %fusion.54, f32[128,6,128]{2,0,1:T(8,128)S(1)} %bitcast.241), kind=kLoop, calls=%fused_computation.30 | loop fusion | flops 2359296 | bytes 10223688 | tf_op jit(solution)/shard_map/jit(_where)/select_n | solution.py:239
  243.6 5.5 %collective-permute-done.14 = bf16[2,14,128,128]{3,2,1,0:T(8,128)(2,1)} collective-permute-done((bf16[2,14,128,128]{3,2,1,0:T(8,128)(2,1)}, bf16[2,14,128,128]{3,2,1,0:T(8,128)(2,1)}, u32[]{:S(2)}, u32[]{:S(2)}) %collective-permute-start.14) | collective-permute-done | bytes 917536 | tf_op jit(solution)/shard_map/ppermute | solution.py:156
  249.1 18.2 %collective-permute-done.15 = bf16[2,14,128,128]{3,2,1,0:T(8,128)(2,1)} collective-permute-done((bf16[2,14,128,128]{3,2,1,0:T(8,128)(2,1)}, bf16[2,14,128,128]{3,2,1,0:T(8,128)(2,1)}, u32[]{:S(2)}, u32[]{:S(2)}) %collective-permute-start.15) | collective-permute-done | bytes 917536 | tf_op jit(solution)/shard_map/ppermute | solution.py:156
  269.4 2.9 pad_maximum_fusion.ad_ref
  272.3 5.5 %pad_maximum_fusion.1.be_ref = bf16[2,2,42,128,128]{4,3,2,1,0:T(8,128)(2,1)} fusion(bf16[1,2,42,128,128]{4,3,2,1,0:T(8,128)(2,1)} %bitcast.58, bf16[1,2,42,128,128]{4,3,2,1,0:T(8,128)(2,1)} %bitcast.57), kind=kLoop, calls=%fused_computation.18 | loop fusion | flops 2752512 | bytes 11010048 | tf_op jit(solution)/shard_map/stack | solution.py:160
  280.4 3.4 %gather_fusion.16 = f32[12,128,128]{2,1,0:T(8,128)} fusion(f32[8,6,128,128]{3,2,1,0:T(8,128)} %bitcast.242, s32[12]{0:T(128)S(1)} %get-tuple-element.34), kind=kCustom, calls=%fused_computation.16 | custom fusion | bytes 1572960 | tf_op jit(solution)/shard_map/gather | solution.py:218
  283.8 3.4 %gather_fusion.15 = f32[12,128,128]{2,1,0:T(8,128)} fusion(f32[8,6,128,128]{3,2,1,0:T(8,128)} %bitcast.243, s32[12]{0:T(128)S(1)} %get-tuple-element.35), kind=kCustom, calls=%fused_computation.15 | custom fusion | bytes 1572960 | tf_op jit(solution)/shard_map/gather | solution.py:218
  287.2 3.4 %gather_fusion.14 = f32[12,128,128]{2,1,0:T(8,128)} fusion(f32[8,6,128,128]{3,2,1,0:T(8,128)} %bitcast.244, s32[12]{0:T(128)S(1)} %fusion.75), kind=kCustom, calls=%fused_computation.14 | custom fusion | bytes 1572960 | tf_op jit(solution)/shard_map/gather | solution.py:218
  296.7 22.9 %update.1 = (f32[12,6,128,128]{3,2,1,0:T(8,128)}, f32[12,6,128,128]{3,2,1,0:T(8,128)}) custom-call(s32[8]{0:T(128)S(1)} %pad_add_fusion.place, f32[12,6,128,128]{3,2,1,0:T(8,128)} %bitcast.237, f32[12,6,128,128]{3,2,1,0:T(8,128)} %bitcast.239, bf16[12,6,128,128]{3,2,1,0:T(8,128)(2,1)S(1)} %bitcast.200, bf16[12,6,128,128]{3,2,1,0:T(8,128)(2,1)S(1)} %bitcast.201, ...), custom_call_target="tpu_custom_call" | custom-call | tf_op jit(solution)/shard_map/update/pallas_call | solution.py:225
  (229 shorter events, 105.6 us)
Async XLA Ops:
  7.2 48.0 %copy-start = (f32[12,128,128]{2,1,0:T(8,128)S(1)}, f32[12,128,128]{2,1,0:T(8,128)}, u32[]{:S(2)}) copy-start(f32[12,128,128]{2,1,0:T(8,128)} %param.21) | copy-start | bytes 2359300
  7.2 270.6 %all-gather.5.cloned.1.call-start = ((), (), s32[]{:S(2)}) async-start(), calls=%async_computation | async-start | bytes 1966080 | tf_op jit(solution)/shard_map/all_gather | solution.py:209
  7.2 6.5 %copy-start.3 = (bf16[12,128,6,128]{3,1,2,0:T(8,128)(2,1)S(1)}, bf16[12,128,6,128]{3,1,2,0:T(8,128)(2,1)}, u32[]{:S(2)}) copy-start(bf16[12,128,6,128]{3,1,2,0:T(8,128)(2,1)} %param.18) | copy-start | bytes 7077892
  13.7 49.1 %collective-permute-start.1 = (bf16[6,128,128]{2,1,0:T(8,128)(2,1)}, bf16[6,128,128]{2,1,0:T(8,128)(2,1)}, u32[]{:S(2)}, u32[]{:S(2)}) collective-permute-start(bf16[6,128,128]{2,1,0:T(8,128)(2,1)} %gather_fusion.5), channel_id=1, source_target_pairs={{0,1},{1,2},{2,3},{3,4},{4,5},{5,6},{6,7},{7,0},{8,9},{9,10},{10,1... | collective-permute-start | bytes 589832 | tf_op jit(solution)/shard_map/ppermute | solution.py:131
  19.4 45.1 %collective-permute-start = (bf16[2,6,128,128]{3,2,1,0:T(8,128)(2,1)}, bf16[2,6,128,128]{3,2,1,0:T(8,128)(2,1)}, u32[]{:S(2)}, u32[]{:S(2)}) collective-permute-start(bf16[2,6,128,128]{3,2,1,0:T(8,128)(2,1)} %pad_maximum_fusion.14), channel_id=1, source_target_pairs={{0,7},{1,0},{2,1},{3,2},{4,3},{5,4},{6,5},{7,6},{8,15},{9,8},{10,9... | collective-permute-start | bytes 1179656 | tf_op jit(solution)/shard_map/ppermute | solution.py:131
  27.8 45.4 %collective-permute-start.3 = (bf16[6,128,128]{2,1,0:T(8,128)(2,1)}, bf16[6,128,128]{2,1,0:T(8,128)(2,1)}, u32[]{:S(2)}, u32[]{:S(2)}) collective-permute-start(bf16[6,128,128]{2,1,0:T(8,128)(2,1)} %gather_fusion.10), channel_id=1, source_target_pairs={{0,24},{8,0},{16,8},{24,16},{1,25},{9,1},{17,9},{25,17},{2,26},{10... | collective-permute-start | bytes 589832 | tf_op jit(solution)/shard_map/ppermute | solution.py:131
  35.5 37.7 %collective-permute-start.2 = (bf16[2,6,128,128]{3,2,1,0:T(8,128)(2,1)}, bf16[2,6,128,128]{3,2,1,0:T(8,128)(2,1)}, u32[]{:S(2)}, u32[]{:S(2)}) collective-permute-start(bf16[2,6,128,128]{3,2,1,0:T(8,128)(2,1)} %pad_maximum_fusion.15), channel_id=1, source_target_pairs={{0,8},{8,16},{16,24},{24,0},{1,9},{9,17},{17,25},{25,1},{2,10},{10... | collective-permute-start | bytes 1179656 | tf_op jit(solution)/shard_map/ppermute | solution.py:131
  38.6 19.6 %copy-start.33 = (f32[12,128]{1,0:T(8,128)S(1)}, f32[12,128]{1,0:T(8,128)}, u32[]{:S(2)}) copy-start(f32[12,128]{1,0:T(8,128)} %param.24) | copy-start | bytes 18436
  59.3 8.5 %copy-start.5 = (f32[6,128,128]{2,1,0:T(8,128)S(1)}, f32[6,128,128]{2,1,0:T(8,128)}, u32[]{:S(2)}) copy-start(f32[6,128,128]{2,1,0:T(8,128)} %gather_fusion.1) | copy-start | bytes 1179652
  61.9 4.6 %copy-start.24 = (bf16[6,128,128]{2,1,0:T(8,128)(2,1)S(1)}, bf16[6,128,128]{2,1,0:T(8,128)(2,1)}, u32[]{:S(2)}) copy-start(bf16[6,128,128]{2,1,0:T(8,128)(2,1)} %gather_fusion.7) | copy-start | bytes 589828
  71.8 9.1 %copy-start.32 = (bf16[1,2,128,128]{3,2,1,0:T(8,128)(2,1)S(1)}, bf16[1,2,128,128]{3,2,1,0:T(8,128)(2,1)}, u32[]{:S(2)}) copy-start(bf16[1,2,128,128]{3,2,1,0:T(8,128)(2,1)} %slice_bitcast_fusion.41) | copy-start | bytes 196612
  76.3 17.3 %collective-permute-start.4 = (f32[6,128,128]{2,1,0:T(8,128)}, f32[6,128,128]{2,1,0:T(8,128)}, u32[]{:S(2)}, u32[]{:S(2)}) collective-permute-start(f32[6,128,128]{2,1,0:T(8,128)} %convolution_select_fusion.2), channel_id=1, source_target_pairs={{0,24},{8,0},{16,8},{24,16},{1,25},{9,1},{17,9},{25,17},{2,26},{10... | collective-permute-start | bytes 1179656 | tf_op jit(solution)/shard_map/ppermute | solution.py:131
  77.9 14.8 %collective-permute-start.5 = (f32[6,128,128]{2,1,0:T(8,128)}, f32[6,128,128]{2,1,0:T(8,128)}, u32[]{:S(2)}, u32[]{:S(2)}) collective-permute-start(f32[6,128,128]{2,1,0:T(8,128)} %get-tuple-element.26), channel_id=1, source_target_pairs={{0,1},{1,2},{2,3},{3,4},{4,5},{5,6},{6,7},{7,0},{8,9},{9,10},{10,1... | collective-permute-start | bytes 1179656 | tf_op jit(solution)/shard_map/ppermute | solution.py:131
  90.9 18.9 %collective-permute-start.7 = (f32[6,128,128]{2,1,0:T(8,128)}, f32[6,128,128]{2,1,0:T(8,128)S(1)}, u32[]{:S(2)}, u32[]{:S(2)}) collective-permute-start(f32[6,128,128]{2,1,0:T(8,128)} %get-tuple-element.26), channel_id=1, source_target_pairs={{0,2},{1,3},{2,4},{3,5},{4,6},{5,7},{6,0},{7,1},{8,10},{9,11},{10,... | collective-permute-start | bytes 1179656 | tf_op jit(solution)/shard_map/ppermute | solution.py:131
  91.5 17.8 %collective-permute-start.6 = (f32[6,128,128]{2,1,0:T(8,128)}, f32[6,128,128]{2,1,0:T(8,128)S(1)}, u32[]{:S(2)}, u32[]{:S(2)}) collective-permute-start(f32[6,128,128]{2,1,0:T(8,128)} %convolution_select_fusion.2), channel_id=1, source_target_pairs={{0,16},{8,24},{16,0},{24,8},{1,17},{9,25},{17,1},{25,9},{2,18},{10... | collective-permute-start | bytes 1179656 | tf_op jit(solution)/shard_map/ppermute | solution.py:131
  94.9 4.6 %copy-start.12 = (f32[6,128,128]{2,1,0:T(8,128)S(1)}, f32[6,128,128]{2,1,0:T(8,128)}, u32[]{:S(2)}) copy-start(f32[6,128,128]{2,1,0:T(8,128)} %copy-done.11) | copy-start | bytes 1179652
  99.5 4.1 %copy-start.6 = (f32[6,128,128]{2,1,0:T(8,128)S(1)}, f32[6,128,128]{2,1,0:T(8,128)}, u32[]{:S(2)}) copy-start(f32[6,128,128]{2,1,0:T(8,128)} %gather_fusion.4) | copy-start | bytes 1179652
  108.5 12.6 %collective-permute-start.8 = (f32[6,128,128]{2,1,0:T(8,128)S(1)}, f32[6,128,128]{2,1,0:T(8,128)S(1)}, u32[]{:S(2)}, u32[]{:S(2)}) collective-permute-start(f32[6,128,128]{2,1,0:T(8,128)S(1)} %convolution_select_fusion.1), channel_id=1, source_target_pairs={{0,24},{8,0},{16,8},{24,16},{1,25},{9,1},{17,9},{25,17},{2,26},{10... | collective-permute-start | bytes 1179656 | tf_op jit(solution)/shard_map/ppermute | solution.py:131
  108.6 11.5 %collective-permute-start.9 = (f32[6,128,128]{2,1,0:T(8,128)S(1)}, f32[6,128,128]{2,1,0:T(8,128)S(1)}, u32[]{:S(2)}, u32[]{:S(2)}) collective-permute-start(f32[6,128,128]{2,1,0:T(8,128)S(1)} %get-tuple-element.28), channel_id=1, source_target_pairs={{0,1},{1,2},{2,3},{3,4},{4,5},{5,6},{6,7},{7,0},{8,9},{9,10},{10,1... | collective-permute-start | bytes 1179656 | tf_op jit(solution)/shard_map/ppermute | solution.py:131
  111.0 9.2 %copy-start.28 = (bf16[6,128,128]{2,1,0:T(8,128)(2,1)S(1)}, bf16[6,128,128]{2,1,0:T(8,128)(2,1)}, u32[]{:S(2)}) copy-start(bf16[6,128,128]{2,1,0:T(8,128)(2,1)} %gather_fusion.13) | copy-start | bytes 589828
  113.3 7.3 %copy-start.23 = (bf16[6,128,128]{2,1,0:T(8,128)(2,1)S(1)}, bf16[6,128,128]{2,1,0:T(8,128)(2,1)}, u32[]{:S(2)}) copy-start(bf16[6,128,128]{2,1,0:T(8,128)(2,1)} %gather_fusion.11) | copy-start | bytes 589828
  129.2 151.2 %all-gather.7.cloned.1.call-start = ((), (), s32[]{:S(2)}) async-start(), calls=%async_computation.1 | async-start | bytes 3538944 | tf_op jit(solution)/shard_map/all_gather | solution.py:210
  139.4 132.8 %collective-permute-start.16 = (bf16[2,42,128,128]{3,2,1,0:T(8,128)(2,1)}, bf16[2,42,128,128]{3,2,1,0:T(8,128)(2,1)}, u32[]{:S(2)}, u32[]{:S(2)}) collective-permute-start(bf16[2,42,128,128]{3,2,1,0:T(8,128)(2,1)} %maximum_dynamic-update-slice_fusion), channel_id=1, source_target_pairs={{0,8},{8,0},{16,24},{24,16},{1,9},{9,1},{17,25},{25,17},{2,10},{10... | collective-permute-start | bytes 8257544 | tf_op jit(solution)/shard_map/ppermute | solution.py:157
  139.4 132.8 %collective-permute-start.17 = (bf16[2,42,128,128]{3,2,1,0:T(8,128)(2,1)}, bf16[2,42,128,128]{3,2,1,0:T(8,128)(2,1)}, u32[]{:S(2)}, u32[]{:S(2)}) collective-permute-start(bf16[2,42,128,128]{3,2,1,0:T(8,128)(2,1)} %maximum_dynamic-update-slice_fusion), channel_id=1, source_target_pairs={{0,24},{8,16},{16,8},{24,0},{1,25},{9,17},{17,9},{25,1},{2,26},{10... | collective-permute-start | bytes 8257544 | tf_op jit(solution)/shard_map/ppermute | solution.py:158
  150.9 85.5 %copy-start.35 = (s32[6]{0:T(128)S(1)}, s32[6]{0:T(128)}, u32[]{:S(2)}) copy-start(s32[6]{0:T(128)} %constant.136.clone) | copy-start | bytes 76
  151.2 27.6 %collective-permute-start.10 = (bf16[2,14,128,128]{3,2,1,0:T(8,128)(2,1)S(1)}, bf16[2,14,128,128]{3,2,1,0:T(8,128)(2,1)}, u32[]{:S(2)}, u32[]{:S(2)}) collective-permute-start(bf16[2,14,128,128]{3,2,1,0:T(8,128)(2,1)S(1)} %get-tuple-element.23), channel_id=1, source_target_pairs={{0,1},{1,0},{2,3},{3,2},{4,5},{5,4},{6,7},{7,6},{8,9},{9,8},{10,11... | collective-permute-start | bytes 2752520 | tf_op jit(solution)/shard_map/ppermute | solution.py:154
  152.7 51.9 %collective-permute-start.11 = (bf16[2,14,128,128]{3,2,1,0:T(8,128)(2,1)S(1)}, bf16[2,14,128,128]{3,2,1,0:T(8,128)(2,1)}, u32[]{:S(2)}, u32[]{:S(2)}) collective-permute-start(bf16[2,14,128,128]{3,2,1,0:T(8,128)(2,1)S(1)} %get-tuple-element.21), channel_id=1, source_target_pairs={{0,1},{1,0},{2,3},{3,2},{4,5},{5,4},{6,7},{7,6},{8,9},{9,8},{10,11... | collective-permute-start | bytes 2752520 | tf_op jit(solution)/shard_map/ppermute | solution.py:154
  153.3 81.2 %collective-permute-start.12 = (bf16[2,14,128,128]{3,2,1,0:T(8,128)(2,1)S(1)}, bf16[2,14,128,128]{3,2,1,0:T(8,128)(2,1)}, u32[]{:S(2)}, u32[]{:S(2)}) collective-permute-start(bf16[2,14,128,128]{3,2,1,0:T(8,128)(2,1)S(1)} %get-tuple-element.22), channel_id=1, source_target_pairs={{0,1},{1,0},{2,3},{3,2},{4,5},{5,4},{6,7},{7,6},{8,9},{9,8},{10,11... | collective-permute-start | bytes 2752520 | tf_op jit(solution)/shard_map/ppermute | solution.py:154
  178.8 64.8 %collective-permute-start.13 = (bf16[2,14,128,128]{3,2,1,0:T(8,128)(2,1)}, bf16[2,14,128,128]{3,2,1,0:T(8,128)(2,1)}, u32[]{:S(2)}, u32[]{:S(2)}) collective-permute-start(bf16[2,14,128,128]{3,2,1,0:T(8,128)(2,1)} %collective-permute-done.10), channel_id=1, source_target_pairs={{0,2},{1,7},{2,4},{3,1},{4,6},{5,3},{6,0},{7,5},{8,10},{9,15},{10,... | collective-permute-start | bytes 2752520 | tf_op jit(solution)/shard_map/ppermute | solution.py:156
  204.6 44.5 %collective-permute-start.14 = (bf16[2,14,128,128]{3,2,1,0:T(8,128)(2,1)}, bf16[2,14,128,128]{3,2,1,0:T(8,128)(2,1)}, u32[]{:S(2)}, u32[]{:S(2)}) collective-permute-start(bf16[2,14,128,128]{3,2,1,0:T(8,128)(2,1)} %collective-permute-done.11), channel_id=1, source_target_pairs={{0,2},{1,7},{2,4},{3,1},{4,6},{5,3},{6,0},{7,5},{8,10},{9,15},{10,... | collective-permute-start | bytes 2752520 | tf_op jit(solution)/shard_map/ppermute | solution.py:156
  234.5 32.8 %collective-permute-start.15 = (bf16[2,14,128,128]{3,2,1,0:T(8,128)(2,1)}, bf16[2,14,128,128]{3,2,1,0:T(8,128)(2,1)}, u32[]{:S(2)}, u32[]{:S(2)}) collective-permute-start(bf16[2,14,128,128]{3,2,1,0:T(8,128)(2,1)} %collective-permute-done.12), channel_id=1, source_target_pairs={{0,2},{1,7},{2,4},{3,1},{4,6},{5,3},{6,0},{7,5},{8,10},{9,15},{10,... | collective-permute-start | bytes 2752520 | tf_op jit(solution)/shard_map/ppermute | solution.py:156
  296.7 22.9 %copy-start.1 = (f32[12,128,128]{2,1,0:T(8,128)S(1)}, f32[12,128,128]{2,1,0:T(8,128)}, u32[]{:S(2)}) copy-start(f32[12,128,128]{2,1,0:T(8,128)} %param.21) | copy-start | bytes 2359300
  (27 other events, 66.4 us)
Sparse Core Ops, SparseCore 0:
  129.4 25.0 all-gather.4
  156.7 111.0 all-gather.6
where the time goes:
time: 332 us; the launch traced here: 326 us
  waiting for transfers between devices  102 us (31%)
  local copies, waits for them, and re-layouts  92.3 us (28%)
  other arithmetic  36.4 us (11%)
  matrix products  35.1 us (11%)
  Pallas kernels  22.9 us (7%)
  starting transfers between devices  22.1 us (7%)
  between operations  15.2 us (5%)
    ppermute x3, waiting for transfers between devices, body(): got = lax.ppermute(pack_ad[:, lo:hi], 'col', swap_col)  73 us
    another operation x24, local copies, waits for them, and re-layouts, pack(): tiles = [jnp.stack([left[:n, b], right[:n, b]]) for b, n in enumerate(tall)]  26.2 us
    ppermute x3, waiting for transfers between devices, body(): relayed.append(lax.ppermute(got, 'col', relay_col))  23.7 us
    pallas_call x1, Pallas kernels, body(): pl.pallas_call(functools.partial(update_kernel, count_rows, count_cols),...  22.9 us
    dot_general x25, matrix products, product(): jnp.einsum('bij,bjk->bik', left, right, precision=lax.Precision.HIGHEST)  18.6 us
    unnamed x82, local copies, waits for them, and re-layouts  13.7 us
    gather x4, local copies, waits for them, and re-layouts, body(): own_a, own_d, own_b, own_e = [x[mine, slots] for x in (a, d, b, e)]  11.8 us
    gather x3, local copies, waits for them, and re-layouts, body(): every_l[at % count_cols, at // count_cols]  10.2 us
  transfers between devices with their start and end apart: 20, of which 6 were waited for; matrix products, arithmetic and copies ran while one was open for 40% of the time, Pallas kernels for 0%

commit v1 on v0

v1 whole, which is shorter than its diff:
```python
import functools
import math

import jax
import jax.numpy as jnp
from jax import lax
from jax.experimental import pallas as pl
from jax.experimental.pallas import tpu as pltpu
from jax.sharding import PartitionSpec as P

TILE = 128
MESH = pl.DeviceIdType.MESH
EARLY_SENDS = {"ahead": 2, "level": 7, "behind": 12}
EARLY_RELAYS = {"ahead": 0, "level": 1, "behind": 4}
LAG = 16
WRAP_LAG = 9
HANDLE_AT = {"ahead": 6, "level": 9, "behind": 13}
HANDLE_HOP = 3
IN_FLIGHT = 3


def heights(rows_dev, cols_dev, count_rows, count_cols):
    return [min(rows_dev, (b * count_cols + count_cols - 1) // count_rows + 1) for b in range(cols_dev)]


def split(value):
    hi = value.astype(jnp.bfloat16)
    return hi, (value - hi.astype(jnp.float32)).astype(jnp.bfloat16)


def dot(left, right):
    return jnp.dot(left, right, preferred_element_type=jnp.float32)


def product(left, right):
    left_hi, left_lo = split(left)
    right_hi, right_lo = split(right)
    return dot(
        jnp.concatenate([left_hi, left_lo, left_hi], axis=1), jnp.concatenate([right_hi, right_hi, right_lo], axis=0)
    )


def half_product(exact, value):
    return dot(jnp.concatenate([exact, exact], axis=1), jnp.concatenate(split(value), axis=0))


def product_half(value, exact):
    return dot(jnp.concatenate(split(value), axis=1), jnp.concatenate([exact, exact], axis=0))


def kernel(
    count_rows, count_cols, unit, tall,
    c_in, f_in, a_in, d_in, b_in, e_in, dinv_in, vec_left_in, back_left_in, eig_left_ref, inv_e_in, vec_right_in, back_right_in, eig_right_ref,
    c_ref, f_ref, r_out, l_out,
    a_ref, d_ref, b_ref, e_ref, ad_buf, be_buf, r_buf, l_buf, r_cat, l_cat,
    front_c, front_f, inv_d, vec_left, back_left, inv_e, vec_right, back_right, a_diag, e_diag, ad_right, be_up,
    ad_send, ad_recv, be_send, be_recv, r_send, r_recv, l_send, l_own_send, l_recv, small_send, small_recv, load_sem,
):
    rows_dev, cols_dev = c_ref.shape[:2]
    blocks = rows_dev * count_rows
    row, col = lax.axis_index("row"), lax.axis_index("col")
    pieces = [n // unit for n in tall]
    offsets = [sum(pieces[:b]) for b in range(cols_dev)]
    chunks = sum(pieces)

    def where_is(n):
        b = sum((n >= offset).astype(jnp.int32) for offset in offsets[1:]) if cols_dev > 1 else jnp.int32(0)
        return b, n - pick(b, offsets)

    def pick(b, values):
        out = jnp.int32(values[0])
        for k in range(1, len(values)):
            out = jnp.where(b == k, values[k], out)
        return out

    def chunk_of(b, q):
        return pick(b, offsets) + jnp.minimum(q, pick(b, pieces) - 1)

    phase = lax.rem(col - row + count_rows, count_rows)
    ahead, level, behind = phase == count_rows - 1, phase == 0, phase == 1
    active = ahead | level | behind
    feeder = (phase == 1) | (phase == 2)
    front = jnp.where(ahead, 1, -phase)
    mine, valid = [], []
    for b in range(cols_dev):
        i = b * count_cols + col + front
        valid.append(active & (i >= 0) & (i < blocks))
        mine.append(jnp.clip(i, 0, blocks - 1) // count_rows)

    partner_row = row + 1 - 2 * lax.rem(row, 2)
    cross_row = lax.rem(row + jnp.where(lax.rem(row, 2) == 0, count_rows - 1, 1), count_rows)
    partner_col = col + 1 - 2 * lax.rem(col, 2)
    relay_col = lax.rem(col + jnp.where(lax.rem(col, 2) == 0, 2, count_cols - 2), count_cols)
    even_col = lax.rem(col, 2) == 0
    left_col, right_col = lax.rem(col + count_cols - 1, count_cols), lax.rem(col + 1, count_cols)
    up_row, down_row = lax.rem(row + count_rows - 1, count_rows), lax.rem(row + 1, count_rows)

    def phase_of(r, c):
        return lax.rem(c - r + count_rows, count_rows)

    def is_active(r, c):
        p = phase_of(r, c)
        return (p == count_rows - 1) | (p == 0) | (p == 1)

    def remote(src, dst, send, recv, r, c):
        return pltpu.make_async_remote_copy(
            src_ref=src, dst_ref=dst, send_sem=send, recv_sem=recv, device_id=(r, c), device_id_type=MESH
        )

    def local(src, dst, sem):
        return pltpu.make_async_copy(src, dst, sem)

    solve_loads = []
    for b in range(cols_dev):
        for k, (src, dst) in enumerate([(c_in, front_c), (f_in, front_f)]):
            solve_loads.append(local(src.at[mine[b], b], dst.at[b], load_sem.at[k]))
        for k, (src, dst) in enumerate([(dinv_in, inv_d), (vec_left_in, vec_left), (back_left_in, back_left)]):
            solve_loads.append(local(src.at[mine[b]], dst.at[b], load_sem.at[2 + k]))
    fixed_loads = [
        local(src, dst, load_sem.at[5 + k])
        for k, (src, dst) in enumerate([(inv_e_in, inv_e), (vec_right_in, vec_right), (back_right_in, back_right)])
    ]
    for copy in solve_loads + fixed_loads:
        copy.start()

    barrier = pltpu.get_barrier_semaphore()
    for k in range(1, count_rows):
        pl.semaphore_signal(barrier, inc=1, device_id=(lax.rem(row + k, count_rows), col), device_id_type=MESH)
    for k in range(1, count_cols):
        pl.semaphore_signal(barrier, inc=1, device_id=(row, lax.rem(col + k, count_cols)), device_id_type=MESH)
    pl.semaphore_wait(barrier, count_rows + count_cols - 2)

    @pl.when(level)
    def _():
        for b in range(cols_dev):
            local(a_in.at[mine[b], b], a_diag.at[b], small_recv.at[0]).start()
            local(e_in.at[mine[b], b], e_diag.at[b], small_recv.at[1]).start()
        for b in range(cols_dev):
            at = b - (col == 0).astype(jnp.int32)

            @pl.when(at >= 0)
            def _():
                remote(a_in.at[mine[b], b], a_diag.at[jnp.maximum(at, 0)], small_send.at[0], small_recv.at[0], row, left_col).start()

            to = b + (col == count_cols - 1).astype(jnp.int32)

            @pl.when(to < cols_dev)
            def _():
                remote(a_in.at[mine[b], b], a_diag.at[jnp.minimum(to, cols_dev - 1)], small_send.at[1], small_recv.at[0], row, right_col).start()

            remote(e_in.at[mine[b], b], e_diag.at[b], small_send.at[2], small_recv.at[1], down_row, col).start()
            remote(e_in.at[mine[b], b], e_diag.at[b], small_send.at[3], small_recv.at[1], up_row, col).start()

    @pl.when(feeder)
    def _():
        for b in range(cols_dev):
            at = b - (col == 0).astype(jnp.int32)

            @pl.when(at >= 0)
            def _():
                for k, src in enumerate((a_in, d_in)):
                    remote(src.at[mine[b], b], ad_right.at[jnp.maximum(at, 0), k], small_send.at[4], small_recv.at[2], row, left_col).start()

            for k, src in enumerate((b_in, e_in)):
                remote(src.at[mine[b], b], be_up.at[b, k], small_send.at[5], small_recv.at[3], down_row, col).start()

    def swap(n):
        b, q = where_is(n)
        for k, src in enumerate((a_in, d_in)):
            remote(src.at[pl.ds(q * unit, unit), b], ad_buf.at[0, n, k], ad_send.at[0, n], ad_recv.at[0, n], row, partner_col).start()

    def cross(n):
        b, q = where_is(n)
        for k, src in enumerate((b_in, e_in)):
            remote(src.at[pl.ds(q * unit, unit), b], be_buf.at[1, n, k], be_send.at[1, n], be_recv.at[1, n], cross_row, col).start()

    def near(n):
        b, q = where_is(n)
        for k, src in enumerate((b_in, e_in)):
            remote(src.at[pl.ds(q * unit, unit), b], be_buf.at[0, n, k], be_send.at[0, n], be_recv.at[0, n], partner_row, col).start()

    def whole_ad(side, n):
        return remote(ad_buf.at[side, n], ad_buf.at[side, n], ad_send.at[side, n], ad_recv.at[side, n], row, partner_col)

    def whole_be(side, n):
        return remote(be_buf.at[side, n], be_buf.at[side, n], be_send.at[side, n], be_recv.at[side, n], partner_row, col)

    def relay_sent(n):
        b, _ = where_is(n)
        skip = ((col == count_cols - 2) & (b == cols_dev - 1)) | ((col == 1) & (b == 0))
        return jnp.logical_not(skip)

    def relay(n):
        whole_ad(0, n).wait_recv()

        @pl.when(relay_sent(n))
        def _():
            remote(ad_buf.at[0, n], ad_buf.at[1, n], ad_send.at[1, n], ad_recv.at[1, n], row, relay_col).start()

    def loop(lo, hi, body):
        lax.fori_loop(lo, hi, lambda n, _: (body(n), 0)[1], 0)

    early = jnp.int32(min(IN_FLIGHT, chunks))
    sent = jnp.int32(0)
    for name, flag in (("ahead", ahead), ("level", level), ("behind", behind)):
        early = jnp.where(flag, min(EARLY_SENDS[name], chunks), early)
        sent = jnp.where(flag, min(EARLY_RELAYS[name], chunks), sent)

    wraps = (col == 1) | (col == count_cols - 2)
    sent = jnp.where(wraps, 0, sent)
    loop(0, early, swap)
    loop(0, early, cross)
    loop(0, chunks, near)
    big_loads = [
        local(src, dst, load_sem.at[8 + k])
        for k, (src, dst) in enumerate([(a_in, a_ref), (d_in, d_ref), (b_in, b_ref), (e_in, e_ref), (c_in, c_ref), (f_in, f_ref)])
    ]
    for copy in big_loads:
        copy.start()
    loop(0, sent, relay)

    for k, dst in enumerate((front_c, front_f, inv_d, vec_left, back_left)):
        local(dst, dst, load_sem.at[k]).wait()
    for copy in fixed_loads:
        copy.wait()

    at_last = (col == count_cols - 1).astype(jnp.int32)

    def wait_tiles(ref, sem, short):
        @pl.when(jnp.logical_not(short))
        def _():
            local(ref, ref, sem).wait()

        if cols_dev > 1:

            @pl.when(short)
            def _():
                part = ref.at[pl.ds(0, cols_dev - 1)]
                local(part, part, sem).wait()

    @pl.when(active)
    def _():
        short = (ahead & (col == count_cols - 1)) | (behind & (col == 0))
        wait_tiles(a_diag, small_recv.at[0], short)
        local(e_diag, e_diag, small_recv.at[1]).wait()

    def got_l(c, b):
        back = (c < 0).astype(jnp.int32)
        slot = b - back
        tile = l_buf[lax.rem(c + count_cols, count_cols), jnp.maximum(slot, 0)]
        return jnp.where(slot >= 0, tile, 0.0)

    def wait_r(r):
        remote(r_buf.at[r], r_buf.at[r], r_send.at[0], r_recv.at[r], row, col).wait_recv()

    def wait_l(c):
        remote(l_buf.at[c], l_buf.at[c], l_send.at[0], l_recv.at[c], row, col).wait_recv()

    def direct(src, dst):
        p = phase_of(row, src)
        return (lax.rem(src, 2) == 1) & (dst == lax.rem(src + 1, count_cols)) & ((p == count_rows - 1) | (p == 0))

    def own_routes():
        order = [k for n in range(1, count_cols // 4 + 1) for k in dict.fromkeys((n, count_cols // 2 - n))]
        routes = [(direct(col, right_col), right_col)] + [(None, lax.rem(col + 2 * k, count_cols)) for k in order]
        return routes

    def across(src):
        return (src != col) & (lax.rem(src + col, 2) == 0) & jnp.logical_not(direct(src, partner_col))

    def maybe(when, run):
        return run() if when is None else pl.when(when)(run)

    def send_l(src):
        remote(l_buf.at[src], l_buf.at[src], l_send.at[src], l_recv.at[src], row, partner_col).start()

    def send_own_l():
        send_l(col)
        for k, (when, to) in enumerate(own_routes()):
            maybe(when, lambda: remote(l_buf.at[col], l_buf.at[col], l_own_send.at[k], l_recv.at[col], row, to).start())

    def handle(src):
        wait_l(src)
        pl.when(across(src))(lambda: send_l(src))

    def absorb(ad, be, right, left):
        for b in range(cols_dev):
            a_tile, d_tile = ad(b)
            b_tile, e_tile = be(b)
            value_r, value_l = right(b), left(b)
            front_c[b] = front_c[b] - half_product(a_tile, value_r) + product_half(value_l, b_tile)
            front_f[b] = front_f[b] - half_product(d_tile, value_r) + product_half(value_l, e_tile)

    row_ahead, row_level = lax.rem(col + 1, count_rows), lax.rem(col, count_rows)
    col_first = jnp.where(level, col - 1, col - 2)

    @pl.when(level | behind)
    def _():
        wait_tiles(ad_right, small_recv.at[2], col == count_cols - 1)
        local(be_up, be_up, small_recv.at[3]).wait()
        wait_r(row_ahead)
        handle(lax.rem(col_first + count_cols, count_cols))

        def right_tiles(b):
            tiles = ad_right[b, 0], ad_right[b, 1]
            if b < cols_dev - 1:
                return tiles
            return tuple(jnp.where(col == count_cols - 1, jnp.zeros_like(tile), tile) for tile in tiles)

        absorb(right_tiles, lambda b: (be_up[b, 0], be_up[b, 1]), lambda b: r_buf[row_ahead, b], lambda b: got_l(col_first, b))

    @pl.when(behind)
    def _():
        for copy in big_loads[:4]:
            copy.wait()
        wait_r(row_level)
        handle(left_col)
        absorb(
            lambda b: (a_ref[mine[b], b], d_ref[mine[b], b]),
            lambda b: (b_ref[mine[b], b], e_ref[mine[b], b]),
            lambda b: r_buf[row_level, b],
            lambda b: got_l(col - 1, b),
        )

    @pl.when(active)
    def _():
        span = range(cols_dev)
        coupled = [half_product(a_diag[b], inv_d[b]) for b in span]
        merged = [front_c[b] - product(coupled[b], front_f[b]) for b in span]
        merged = [product(merged[b], inv_e[b]) for b in span]
        spectral = [product(back_left[b], merged[b]) for b in span]
        spectral = [product(spectral[b], vec_right[b]) for b in span]
        for b in span:
            eig = jnp.broadcast_to(eig_left_ref[pl.ds(mine[b], 1), :], (TILE, TILE)).T
            spectral[b] = spectral[b] / (eig - eig_right_ref[pl.ds(b, 1), :])
        new_l = [product(vec_left[b], spectral[b]) for b in span]
        new_l = [product(new_l[b], back_right[b]) for b in span]
        for b in span:
            l_buf[col, b] = jnp.where(valid[b], new_l[b], 0.0)
        summed = [front_f[b] + product_half(new_l[b], e_diag[b]) for b in span]
        for b in span:
            r_buf[row, b] = jnp.where(valid[b], product(inv_d[b], summed[b]), 0.0)

        for k in range(1, count_rows):
            to = lax.rem(row + count_rows - k, count_rows)
            remote(r_buf.at[row], r_buf.at[row], r_send.at[k], r_recv.at[row], to, col).start()
        send_own_l()

    loop(early, chunks, cross)

    lag = min(LAG, chunks - 1)

    def handled(src):
        before = ((level | behind) & (src == left_col)) | (behind & (src == lax.rem(col + count_cols - 2, count_cols)))
        return before | (src == col) | jnp.logical_not(is_active(row, src))

    def handle_at(src):
        p = phase_of(row, src)
        base = jnp.where(p == count_rows - 1, HANDLE_AT["ahead"], jnp.where(p == 0, HANDLE_AT["level"], HANDLE_AT["behind"]))
        return jnp.minimum(base + jnp.where(lax.rem(src + col, 2) == 0, 0, HANDLE_HOP), lag)

    def collect():
        for offset in range(1, -2, -1):
            src = lax.rem(col + offset + count_rows, count_rows)
            taken = ((level | behind) & (src == row_ahead)) | (behind & (src == row_level)) | (src == row)

            @pl.when(jnp.logical_not(taken))
            def _():
                wait_r(src)

        for b in range(cols_dev):
            for k, offset in enumerate((1, 0, -1)):
                hi, lo = split(r_buf[lax.rem(col + offset + count_rows, count_rows), b])
                r_cat[b, k * TILE : (k + 1) * TILE, :TILE] = hi
                r_cat[b, k * TILE : (k + 1) * TILE, TILE:] = lo

        def gather(a):
            for k, offset in enumerate((1, 0, -1)):
                m = a * count_rows + row - offset
                at = jnp.clip(m, 0, blocks - 1)
                tile = l_buf[lax.rem(at, count_cols), at // count_cols]
                hi, lo = split(jnp.where((m >= 0) & (m < blocks), tile, 0.0))
                l_cat[a, :TILE, k * TILE : (k + 1) * TILE] = hi
                l_cat[a, TILE:, k * TILE : (k + 1) * TILE] = lo

        loop(0, rows_dev, gather)

        @pl.when(jnp.logical_not(behind))
        def _():
            for copy in big_loads[:4]:
                copy.wait()

        for copy in big_loads[4:]:
            copy.wait()

    right_side, left_side = lax.rem(col, 2), 1 - lax.rem(col, 2)
    up_side, down_side = 1 - lax.rem(row, 2), lax.rem(row, 2)
    first_relay = jnp.where(col == count_cols - 1, offsets[1] if cols_dev > 1 else chunks, 0)

    def right_chunk(b, q):
        slot = jnp.minimum(b + at_last, cols_dev - 1)
        return chunk_of(slot, q)

    def left_chunk(b, q):
        slot = jnp.maximum(b - (col == 0).astype(jnp.int32), 0)
        return chunk_of(slot, q)

    def need(m):
        b, q = where_is(m)
        at = jnp.where(even_col, left_chunk(b, q), right_chunk(b, q))
        return jnp.where((col == count_cols - 1) & (b == cols_dev - 1), chunks - 1, at)

    def be_tile(side, which, b, a, height):
        at = jnp.clip(a, 0, height - 1)
        return be_buf[side, pick(b, offsets) + at // unit, which, lax.rem(at, unit)]

    def update(m):
        b, q = where_is(m)
        height = pick(b, tall)
        whole_be(0, m).wait_recv()
        lo = jnp.where(m == 0, 0, jnp.minimum(m + 1, chunks))
        loop(lo, jnp.minimum(m + 2, chunks), lambda n: whole_be(1, n).wait_recv())
        lo = jnp.where(m == 0, first_relay, need(jnp.maximum(m - 1, 0)) + 1)
        loop(lo, need(m) + 1, lambda n: whole_ad(1, n).wait_recv())
        at_right, at_left = right_chunk(b, q), left_chunk(b, q)
        j = b * count_cols + col
        for t in range(unit):
            a = q * unit + t
            i = a * count_rows + row
            up_a, down_a = a - (row == 0).astype(jnp.int32), a + (row == count_rows - 1).astype(jnp.int32)

            def apply(near_edge):
                def masked(tile, keep):
                    return jnp.where(keep, tile, jnp.zeros_like(tile)) if near_edge else tile

                def wide(which, own):
                    return jnp.concatenate(
                        [
                            ad_buf[right_side, at_right, which, t],
                            masked(own[a, b], i < j),
                            masked(ad_buf[left_side, at_left, which, t], i < j - 1),
                        ],
                        axis=1,
                    )

                def high(which, own):
                    return jnp.concatenate(
                        [
                            be_tile(up_side, which, b, up_a, height),
                            masked(own[a, b], i < j),
                            masked(be_tile(down_side, which, b, down_a, height), i < j - 1),
                        ],
                        axis=0,
                    )

                first = dot(jnp.concatenate([wide(0, a_ref), wide(1, d_ref)], axis=0), r_cat[b])
                second = dot(l_cat[a], jnp.concatenate([high(0, b_ref), high(1, e_ref)], axis=1))
                c_ref[a, b] = c_ref[a, b] - (first[:TILE, :TILE] + first[:TILE, TILE:]) + (second[:TILE, :TILE] + second[TILE:, :TILE])
                f_ref[a, b] = f_ref[a, b] - (first[TILE:, :TILE] + first[TILE:, TILE:]) + (second[:TILE, TILE:] + second[TILE:, TILE:])

            pl.when(i < j - 1)(lambda: apply(False))
            pl.when((i == j) | (i == j - 1))(lambda: apply(True))

    def done_by(n):
        return jnp.clip((n - lag + 1) * 3, 0, jnp.maximum(n - 1, 0))

    def wrapped_by(n):
        return jnp.where(wraps, jnp.clip((n - min(WRAP_LAG, chunks - 1) + 1) * 2, 0, jnp.maximum(n + 1, 0)), 0)

    def main(n):
        loop(jnp.maximum(early, jnp.where(n == 0, 0, n + IN_FLIGHT)), jnp.minimum(n + IN_FLIGHT + 1, chunks), swap)
        pl.when((n >= sent) & jnp.logical_not(wraps))(lambda: relay(n))
        loop(wrapped_by(n - 1), wrapped_by(n), relay)
        loop(0, count_cols, lambda src: pl.when((n == handle_at(src)) & jnp.logical_not(handled(src)))(lambda: handle(src)))
        pl.when(n == lag)(collect)
        loop(done_by(n - 1), done_by(n), update)

    loop(0, chunks, main)
    loop(wrapped_by(chunks - 1), jnp.where(wraps, chunks, 0), relay)
    loop(done_by(chunks - 1), chunks, update)

    copies = [local(r_buf.at[row], r_out, load_sem.at[14]), local(l_buf.at[col], l_out, load_sem.at[15])]
    for copy in copies:
        copy.start()

    def drain(n):
        whole_ad(0, n).wait_send()
        pl.when(relay_sent(n))(lambda: whole_ad(1, n).wait_send())
        whole_be(0, n).wait_send()
        whole_be(1, n).wait_send()

    loop(0, chunks, drain)

    def wait_sent(ref, sem):
        remote(ref, ref, sem, r_recv.at[0], row, col).wait_send()

    def wait_tiles_sent(ref, sem, short):
        pl.when(jnp.logical_not(short))(lambda: wait_sent(ref, sem))
        if cols_dev > 1:
            pl.when(short)(lambda: wait_sent(ref.at[pl.ds(0, cols_dev - 1)], sem))

    @pl.when(level)
    def _():
        wait_tiles_sent(a_diag, small_send.at[0], col == 0)
        wait_tiles_sent(a_diag, small_send.at[1], col == count_cols - 1)
        wait_sent(e_diag, small_send.at[2])
        wait_sent(e_diag, small_send.at[3])

    @pl.when(feeder)
    def _():
        wait_tiles_sent(ad_right, small_send.at[4], col == 0)
        wait_sent(be_up, small_send.at[5])

    @pl.when(active)
    def _():
        for k in range(1, count_rows):
            wait_sent(r_buf.at[row], r_send.at[k])

        for k, (when, _) in enumerate(own_routes()):
            maybe(when, lambda: wait_sent(l_buf.at[col], l_own_send.at[k]))

    def drain_l(src):
        pl.when(is_active(row, src) & ((src == col) | across(src)))(lambda: wait_sent(l_buf.at[src], l_send.at[src]))

    loop(0, count_cols, drain_l)

    for copy in copies:
        copy.wait()


def body(*args):
    count_rows = lax.axis_size("row")
    count_cols = lax.axis_size("col")
    row, col = lax.axis_index("row"), lax.axis_index("col")
    wide = [x.transpose(0, 2, 1, 3) for x in args[:6]]
    rows_dev, cols_dev = wide[0].shape[:2]
    blocks = rows_dev * count_rows
    tall = heights(rows_dev, cols_dev, count_rows, count_cols)
    unit = math.gcd(*tall)
    chunks = sum(tall) // unit
    anywhere, inside = pl.BlockSpec(memory_space=pl.ANY), pl.BlockSpec(memory_space=pltpu.VMEM)
    whole, few = (rows_dev, cols_dev, TILE, TILE), (cols_dev, TILE, TILE)
    f32, bf16 = jnp.float32, jnp.bfloat16
    dma = pltpu.SemaphoreType.DMA
    new_c, new_f, new_r, new_l = pl.pallas_call(
        functools.partial(kernel, count_rows, count_cols, unit, tall),
        in_specs=[anywhere] * 9 + [inside] + [anywhere] * 3 + [inside],
        out_specs=[inside, inside, anywhere, anywhere],
        out_shape=[jax.ShapeDtypeStruct(whole, f32)] * 2 + [jax.ShapeDtypeStruct(few, f32)] * 2,
        scratch_shapes=[pltpu.VMEM(whole, bf16)] * 4
        + [pltpu.VMEM((2, chunks, 2, unit, TILE, TILE), bf16)] * 2
        + [
            pltpu.VMEM((count_rows,) + few, f32),
            pltpu.VMEM((count_cols,) + few, f32),
            pltpu.VMEM((cols_dev, 3 * TILE, 2 * TILE), bf16),
            pltpu.VMEM((rows_dev, 2 * TILE, 3 * TILE), bf16),
        ]
        + [pltpu.VMEM(few, f32)] * 8
        + [pltpu.VMEM(few, bf16)] * 2
        + [pltpu.VMEM((cols_dev, 2, TILE, TILE), bf16)] * 2
        + [dma((2, chunks))] * 4
        + [dma((count_rows,)), dma((count_rows,)), dma((count_cols,)), dma((count_cols,)), dma((count_cols,)), dma((6,)), dma((4,)), dma((16,))],
        compiler_params=pltpu.CompilerParams(collective_id=0, has_side_effects=True, vmem_limit_bytes=60 * 1024 * 1024),
        name="fronts",
    )(*wide, *args[6:])

    phase = (col - row) % count_rows
    front = jnp.where(phase == count_rows - 1, 1, -phase)
    active = (phase == count_rows - 1) | (phase <= 1)
    at = jnp.arange(cols_dev, dtype=jnp.int32) * count_cols + col + front
    i = jnp.arange(rows_dev, dtype=jnp.int32)[:, None] * count_rows + row
    here = (active & (i == at[None, :]))[:, :, None, None]
    out_r = jnp.where(here, new_r[None], 0.0)
    out_l = jnp.where(here, new_l[None], 0.0)
    return tuple(x.transpose(0, 2, 1, 3) for x in (new_c, new_f, out_r, out_l))


def solution(mesh):
    grid = P(None, "row", None, "col")
    left, right = P(None, "row", None), P(None, "col", None)
    in_specs = (grid,) * 6 + (left,) * 3 + (P(None, "row"),) + (right,) * 3 + (P(None, "col"),)
    return jax.shard_map(body, mesh=mesh, in_specs=in_specs, out_specs=(grid,) * 4, check_vma=False)
```

time: 332 us -> 152 us (0.46)
  the two profiles are of different devices: /device:TPU:28 before, /device:TPU:26 now
where the time goes in v1:
time: 152 us
  Pallas kernels  138 us (91%)
  other arithmetic  6.3 us (4%)
  local copies, waits for them, and re-layouts  6.23 us (4%)
    pallas_call x1, Pallas kernels, body(): pl.pallas_call(functools.partial(kernel, count_rows, count_cols, unit, ta...  138 us
    unnamed x6, local copies, waits for them, and re-layouts  6.23 us
    select_n x1, other arithmetic, body(): out_l = jnp.where(here, new_l[None], 0.0)  6.21 us

profile of v1, /device:TPU:26, one launch (start us, length us, event | category | flops | bytes accessed | tf_op | source)
XLA Modules:
  0.0 151.5 jit_solution(10893750730189812813)
XLA Ops:
  0.7 0.1 compare_and_fusion
  0.8 138.3 %fronts.1 = (f32[12,6,128,128]{3,2,1,0:T(8,128)}, f32[12,6,128,128]{3,2,1,0:T(8,128)}, f32[6,128,128]{2,1,0:T(8,128)}, f32[6,128,128]{2,1,0:T(8,128)}) custom-call(f32[12,6,128,128]{3,2,1,0:T(8,128)} %bitcast.12, f32[12,6,128,128]{3,2,1,0:T(8,128)} %bitcast.13, bf16[12,6,128,128]{3,2,1,0:T(8,128)(2,1)} %bitcast.14, bf16[12,6,128,128]{3,2,1,0:T(8,128)(2,1)} %bitcast.15, ...), custom_call_target="tpu_custom_call" | custom-call | tf_op jit(solution)/shard_map/fronts/pallas_call | solution.py:545
  139.1 0.0 copy-start.1
  139.1 6.2 %broadcast_select_fusion = (f32[12,128,6,128]{3,1,2,0:T(8,128)}, f32[12,128,6,128]{3,1,2,0:T(8,128)}) fusion(f32[128,6,128]{2,0,1:T(8,128)} %bitcast.19, pred[12,6]{1,0:T(8,128)(4,1)S(1)} %compare_and_fusion, f32[128,6,128]{2,0,1:T(8,128)} %bitcast.18), kind=kLoop, calls=%fused_computation | loop fusion | flops 2359296 | bytes 10223688 | tf_op jit(solution)/shard_map/jit(_where)/select_n | solution.py:574
  145.3 0.0 copy-done.1
  145.3 0.0 copy-start
  145.3 2.4 %copy.20 = f32[12,128,6,128]{3,1,2,0:T(8,128)} copy(f32[12,128,6,128]{3,1,2,0:T(8,128)S(1)} %bitcast.11) | data formatting | bytes 9437184
  147.7 1.6 %copy-done = f32[12,6,128,128]{3,2,1,0:T(8,128)S(1)} copy-done((f32[12,6,128,128]{3,2,1,0:T(8,128)S(1)}, f32[12,6,128,128]{3,2,1,0:T(8,128)}, u32[]{:S(2)}) %copy-start) | copy-done | bytes 4718616
  149.3 2.2 %copy.21 = f32[12,128,6,128]{3,1,2,0:T(8,128)} copy(f32[12,128,6,128]{3,1,2,0:T(8,128)S(1)} %bitcast.10) | data formatting | bytes 9437184
  (2 shorter events, 0.0 us)
Async XLA Ops:
  139.1 6.2 %copy-start.1 = (f32[12,6,128,128]{3,2,1,0:T(8,128)S(1)}, f32[12,6,128,128]{3,2,1,0:T(8,128)}, u32[]{:S(2)}) copy-start(f32[12,6,128,128]{3,2,1,0:T(8,128)} %get-tuple-element.8) | copy-start | bytes 14155780
  145.3 4.0 %copy-start = (f32[12,6,128,128]{3,2,1,0:T(8,128)S(1)}, f32[12,6,128,128]{3,2,1,0:T(8,128)}, u32[]{:S(2)}) copy-start(f32[12,6,128,128]{3,2,1,0:T(8,128)} %get-tuple-element.9) | copy-start | bytes 14155780

commit v2 on v1

--- a/solution.py
+++ b/solution.py
@@ -16,7 +16,7 @@
 WRAP_LAG = 9
 HANDLE_AT = {"ahead": 6, "level": 9, "behind": 13}
 HANDLE_HOP = 3
-IN_FLIGHT = 3
+IN_FLIGHT = 5
 
 
 def heights(rows_dev, cols_dev, count_rows, count_cols):
@@ -526,6 +526,18 @@
 
     for copy in copies:
         copy.wait()
+
+
+def place_kernel(count_rows, count_cols, r_ref, l_ref, r_out, l_out):
+    cols_dev = r_out.shape[1]
+    row, col = lax.axis_index("row"), lax.axis_index("col")
+    phase = lax.rem(col - row + count_rows, count_rows)
+    active = (phase == count_rows - 1) | (phase <= 1)
+    front = jnp.where(phase == count_rows - 1, 1, -phase)
+    for b in range(cols_dev):
+        here = active & (pl.program_id(0) * count_rows + row == b * count_cols + col + front)
+        r_out[0, b] = jnp.where(here, r_ref[b], 0.0)
+        l_out[0, b] = jnp.where(here, l_ref[b], 0.0)
 
 
 def body(*args):
@@ -546,7 +558,7 @@
         functools.partial(kernel, count_rows, count_cols, unit, tall),
         in_specs=[anywhere] * 9 + [inside] + [anywhere] * 3 + [inside],
         out_specs=[inside, inside, anywhere, anywhere],
-        out_shape=[jax.ShapeDtypeStruct(whole, f32)] * 2 + [jax.ShapeDtypeStruct(few, f32)] * 2,
+        out_shape=[pltpu.VMEM(whole, f32)] * 2 + [jax.ShapeDtypeStruct(few, f32)] * 2,
         scratch_shapes=[pltpu.VMEM(whole, bf16)] * 4
         + [pltpu.VMEM((2, chunks, 2, unit, TILE, TILE), bf16)] * 2
         + [
@@ -560,18 +572,19 @@
         + [pltpu.VMEM((cols_dev, 2, TILE, TILE), bf16)] * 2
         + [dma((2, chunks))] * 4
         + [dma((count_rows,)), dma((count_rows,)), dma((count_cols,)), dma((count_cols,)), dma((count_cols,)), dma((6,)), dma((4,)), dma((16,))],
-        compiler_params=pltpu.CompilerParams(collective_id=0, has_side_effects=True, vmem_limit_bytes=60 * 1024 * 1024),
+        compiler_params=pltpu.CompilerParams(collective_id=0, has_side_effects=True, vmem_limit_bytes=48 * 1024 * 1024),
         name="fronts",
     )(*wide, *args[6:])
 
-    phase = (col - row) % count_rows
-    front = jnp.where(phase == count_rows - 1, 1, -phase)
-    active = (phase == count_rows - 1) | (phase <= 1)
-    at = jnp.arange(cols_dev, dtype=jnp.int32) * count_cols + col + front
-    i = jnp.arange(rows_dev, dtype=jnp.int32)[:, None] * count_rows + row
-    here = (active & (i == at[None, :]))[:, :, None, None]
-    out_r = jnp.where(here, new_r[None], 0.0)
-    out_l = jnp.where(here, new_l[None], 0.0)
+    out_r, out_l = pl.pallas_call(
+        functools.partial(place_kernel, count_rows, count_cols),
+        grid=(rows_dev,),
+        in_specs=[inside] * 2,
+        out_specs=[pl.BlockSpec((1, cols_dev, TILE, TILE), lambda k: (k, 0, 0, 0))] * 2,
+        out_shape=[jax.ShapeDtypeStruct(whole, f32)] * 2,
+        cost_estimate=pl.CostEstimate(flops=4 * 10**7, bytes_accessed=8 * math.prod(whole), transcendentals=0),
+        name="place",
+    )(new_r, new_l)
     return tuple(x.transpose(0, 2, 1, 3) for x in (new_c, new_f, out_r, out_l))
 
 

time: 152 us -> 138 us (0.908)
  the two profiles are of different devices: /device:TPU:26 before, /device:TPU:28 now
where the time goes in v2:
time: 138 us; the launch traced here: 136 us
  Pallas kernels  131 us (95%)
  local copies, waits for them, and re-layouts  4.37 us (3%)
    pallas_call x1, Pallas kernels, body(): pl.pallas_call(functools.partial(kernel, count_rows, count_cols, unit, ta...  124 us
    pallas_call x1, Pallas kernels, body(): pl.pallas_call(functools.partial(place_kernel, count_rows, count_cols), g...  6.89 us
    unnamed x2, local copies, waits for them, and re-layouts  4.37 us

profile of v2, /device:TPU:28, one launch (start us, length us, event | category | flops | bytes accessed | tf_op | source)
XLA Modules:
  0.0 136.3 jit_solution(7751899376321959049)
XLA Ops:
  0.6 124.4 %fronts.1 = (f32[12,6,128,128]{3,2,1,0:T(8,128)S(1)}, f32[12,6,128,128]{3,2,1,0:T(8,128)S(1)}, f32[6,128,128]{2,1,0:T(8,128)}, f32[6,128,128]{2,1,0:T(8,128)}) custom-call(f32[12,6,128,128]{3,2,1,0:T(8,128)} %bitcast.12, f32[12,6,128,128]{3,2,1,0:T(8,128)} %bitcast.13, bf16[12,6,128,128]{3,2,1,0:T(8,128)(2,1)} %bitcast.14, ...), custom_call_target="tpu_custom_call" | custom-call | tf_op jit(solution)/shard_map/fronts/pallas_call | solution.py:557
  125.0 2.2 %copy.20 = f32[12,128,6,128]{3,1,2,0:T(8,128)} copy(f32[12,128,6,128]{3,1,2,0:T(8,128)S(1)} %bitcast.11) | data formatting | bytes 9437184
  127.2 2.2 %copy.21 = f32[12,128,6,128]{3,1,2,0:T(8,128)} copy(f32[12,128,6,128]{3,1,2,0:T(8,128)S(1)} %bitcast.10) | data formatting | bytes 9437184
  129.4 6.9 %place.1 = (f32[12,6,128,128]{3,2,1,0:T(8,128)}, f32[12,6,128,128]{3,2,1,0:T(8,128)}) custom-call(f32[6,128,128]{2,1,0:T(8,128)} %get-tuple-element.12.r_ref, f32[6,128,128]{2,1,0:T(8,128)} %get-tuple-element.13.l_ref), custom_call_target="tpu_custom_call" | custom-call | flops 40000000 | bytes 9437184 | tf_op jit(solution)/shard_map/place/pallas_call | solution.py:579

commit v3 on v2

--- a/solution.py
+++ b/solution.py
@@ -12,9 +12,9 @@
 MESH = pl.DeviceIdType.MESH
 EARLY_SENDS = {"ahead": 2, "level": 7, "behind": 12}
 EARLY_RELAYS = {"ahead": 0, "level": 1, "behind": 4}
-LAG = 16
+LAG = 15
 WRAP_LAG = 9
-HANDLE_AT = {"ahead": 6, "level": 9, "behind": 13}
+HANDLE_AT = {"ahead": 5, "level": 8, "behind": 12}
 HANDLE_HOP = 3
 IN_FLIGHT = 5
 

time: 138 us -> 139 us (level); the launches traced: 136 us -> 139 us
  Pallas kernels: 131 us -> 134 us
    pallas_call x1, Pallas kernels: 124 us -> 127 us  [body(): pl.pallas_call(functools.partial(kernel, count_rows, count_cols, unit, ta...]
where the time goes in v3:
time: 139 us
  Pallas kernels  134 us (96%)
  local copies, waits for them, and re-layouts  4.37 us (3%)
    pallas_call x1, Pallas kernels, body(): pl.pallas_call(functools.partial(kernel, count_rows, count_cols, unit, ta...  127 us
    pallas_call x1, Pallas kernels, body(): pl.pallas_call(functools.partial(place_kernel, count_rows, count_cols), g...  6.89 us
    unnamed x2, local copies, waits for them, and re-layouts  4.37 us

profile of v3, /device:TPU:28, one launch (start us, length us, event | category | flops | bytes accessed | tf_op | source)
XLA Modules:
  0.0 139.0 jit_solution(13388660981191039754)
XLA Ops:
  0.6 127.1 %fronts.1 = (f32[12,6,128,128]{3,2,1,0:T(8,128)S(1)}, f32[12,6,128,128]{3,2,1,0:T(8,128)S(1)}, f32[6,128,128]{2,1,0:T(8,128)}, f32[6,128,128]{2,1,0:T(8,128)}) custom-call(f32[12,6,128,128]{3,2,1,0:T(8,128)} %bitcast.12, f32[12,6,128,128]{3,2,1,0:T(8,128)} %bitcast.13, bf16[12,6,128,128]{3,2,1,0:T(8,128)(2,1)} %bitcast.14, ...), custom_call_target="tpu_custom_call" | custom-call | tf_op jit(solution)/shard_map/fronts/pallas_call | solution.py:557
  127.7 2.2 %copy.20 = f32[12,128,6,128]{3,1,2,0:T(8,128)} copy(f32[12,128,6,128]{3,1,2,0:T(8,128)S(1)} %bitcast.11) | data formatting | bytes 9437184
  129.9 2.2 %copy.21 = f32[12,128,6,128]{3,1,2,0:T(8,128)} copy(f32[12,128,6,128]{3,1,2,0:T(8,128)S(1)} %bitcast.10) | data formatting | bytes 9437184
  132.1 6.9 %place.1 = (f32[12,6,128,128]{3,2,1,0:T(8,128)}, f32[12,6,128,128]{3,2,1,0:T(8,128)}) custom-call(f32[6,128,128]{2,1,0:T(8,128)} %get-tuple-element.12.r_ref, f32[6,128,128]{2,1,0:T(8,128)} %get-tuple-element.13.l_ref), custom_call_target="tpu_custom_call" | custom-call | flops 40000000 | bytes 9437184 | tf_op jit(solution)/shard_map/place/pallas_call | solution.py:579
